TPU v7x, 32 devices: a whole 2x2x4 slice. The times are simulated.
32 devices in a mesh: groups: 2 (over y), users: 4 (over z), routers: 2 (over x), heads: 2 (over core).
Axes of the slice: x: 2, y: 2, z: 4, core: 2. Of those that a mesh axis runs over, the one named last changes fastest.
Arguments:
- items: bfloat16 [64, 64, 1024], P(('groups', 'users', 'routers')), parts along dimension 0, may hold values from -6 to 6
- block_owner: int32 [64, 1], P(('groups', 'users', 'routers')), parts along dimension 0, may hold values from 0 to 3; in each aligned block of 4 rows (0 to 3, 4 to 7, ...) at most 2 rows name the same one
- block_user: int32 [64], P(('groups', 'users', 'routers')), parts along dimension 0, may hold values from 0 to 1
- block_fill: int32 [64], P(('groups', 'users', 'routers')), parts along dimension 0, may hold values from 1 to 64
- prefix_keys: bfloat16 [16, 256, 1024], P(('groups', 'users'), None, 'heads'), parts along dimension 0, may hold values from -6 to 6
- prefix_values: bfloat16 [16, 256, 1024], P(('groups', 'users'), None, 'heads'), parts along dimension 0, may hold values from -6 to 6
- w_in: bfloat16 [4, 1024, 1024], P(None, 'routers', 'heads'), may hold values from -0.1875 to 0.1875
- attn_gain: bfloat16 [1024], P('heads'), may hold values from 0.25 to 1.75
- w_o: bfloat16 [1024, 1024], P('heads', 'routers'), may hold values from -0.1875 to 0.1875
- mlp_gain: bfloat16 [1024], replicated, may hold values from 0.25 to 1.75
- w_one: bfloat16 [1024, 256], replicated, may hold values from -0.1875 to 0.1875
- w_two: bfloat16 [256], replicated, may hold values from -0.375 to 0.375
Outputs:
- scores: float32 [64, 64], P(('groups', 'users', 'routers')), parts along dimension 0
There are 2 independent parts, one for each index of `groups`. A program takes and returns all parts, laid end to end along the dimension named above; an argument that names none is the same for every part. Nothing has to cross between parts.
Inputs may be any that keep to these rules, and one draw needn't show every extreme that they name: `block_owner`: within the rows of one device (aligned blocks of 4 blocks), no owner is named by more than 2 rows, and in every draw some owner is named by exactly 2 rows of some device.
All inputs are finite; a program needn't handle non-finite values.
Results may differ from a plain program's by a relative error of at most 0.005.
Values may be sent and summed in bfloat16 or wider, within the bound.
A program may use at most 64 MiB of HBM per device.

v0:
```python
import jax
import jax.numpy as jnp
from jax import lax
from jax.sharding import PartitionSpec as P

D = 1024
HEAD_DIM = 128
CAP = 2
HD = 1024
EPSILON = 1e-05


def prefix_attention(group_queries, group_users, prefix_keys, prefix_values):
    group_size, block_width, half_width = group_queries.shape
    heads_here = half_width // HEAD_DIM
    safe_user = jnp.maximum(group_users, 0)
    user_keys = jnp.take(prefix_keys, safe_user, axis=0)
    user_values = jnp.take(prefix_values, safe_user, axis=0)
    query_heads = group_queries.reshape(group_size, block_width, heads_here, HEAD_DIM)
    key_heads = user_keys.reshape(group_size, -1, heads_here, HEAD_DIM)
    value_heads = user_values.reshape(group_size, -1, heads_here, HEAD_DIM)
    raw_scores = jnp.einsum(
        "gqhd,gkhd->ghqk", query_heads, key_heads, preferred_element_type=jnp.float32
    ) * HEAD_DIM ** (-0.5)
    weights = jax.nn.silu(raw_scores).astype(jnp.bfloat16)
    summed = jnp.einsum("ghqk,gkhd->gqhd", weights, value_heads, preferred_element_type=jnp.float32)
    return summed.reshape(group_size, block_width, half_width).astype(jnp.bfloat16)


def local(
    items,
    block_owner,
    block_user,
    block_fill,
    prefix_keys,
    prefix_values,
    w_in,
    attn_gain,
    w_o,
    mlp_gain,
    w_one,
    w_two,
):
    blocks, block_width, model_width = items.shape
    row_count = blocks * block_width
    half_width = w_in.shape[2]
    heads_here = half_width // HEAD_DIM
    peer_count = lax.axis_size("users")
    slot_count = peer_count * CAP
    score_scale = HEAD_DIM ** (-0.5)
    flat_items = items.reshape(row_count, model_width)
    projected = jnp.einsum(
        "rk,pkc->prc",
        flat_items,
        lax.all_gather(w_in, "routers", axis=1, tiled=True),
        preferred_element_type=jnp.float32,
    )
    activated = jax.nn.silu(projected)
    queries = activated[0].astype(jnp.bfloat16)
    target = block_owner[:, 0]
    earlier = lax.broadcasted_iota(jnp.int32, (blocks, blocks), 1) < lax.broadcasted_iota(
        jnp.int32, (blocks, blocks), 0
    )
    same_target = target[:, None] == target[None, :]
    dest_rank = jnp.sum((same_target & earlier).astype(jnp.int32), axis=1)
    position = target * CAP + dest_rank
    selector = lax.broadcasted_iota(jnp.int32, (slot_count, blocks), 0) == position[None, :]
    block_queries = queries.reshape(blocks, block_width * half_width)
    outgoing = jnp.dot(
        selector.astype(jnp.bfloat16), block_queries, preferred_element_type=jnp.float32
    ).astype(jnp.bfloat16)
    outgoing = outgoing.reshape(peer_count, CAP, block_width, half_width)
    slot_user = jnp.sum(jnp.where(selector, block_user[None, :] + 1, 0), axis=1) - 1
    slot_user = slot_user.reshape(peer_count, CAP)
    arrived = lax.all_to_all(outgoing, "users", split_axis=0, concat_axis=0, tiled=True)
    arrived_users = lax.all_to_all(slot_user, "users", split_axis=0, concat_axis=0, tiled=True)
    sources, per_source = arrived_users.shape
    total_slots = sources * per_source
    flat_queries = arrived.reshape(total_slots, block_width, half_width)
    flat_users = arrived_users.reshape(total_slots)
    packing = jnp.argsort((flat_users < 0).astype(jnp.int32), stable=True)
    used_slots = jnp.sum((flat_users >= 0).astype(jnp.int32))
    packed_queries = jnp.take(flat_queries, packing, axis=0)
    packed_users = jnp.take(flat_users, packing, axis=0)
    needed = (used_slots + 3) // 4

    def attend_group(group_index, buffer):
        first_slot = group_index * 4
        group_queries = lax.dynamic_slice_in_dim(packed_queries, first_slot, 4, 0)
        group_users = lax.dynamic_slice_in_dim(packed_users, first_slot, 4, 0)
        result = prefix_attention(group_queries, group_users, prefix_keys, prefix_values)
        return lax.dynamic_update_slice_in_dim(buffer, result, first_slot, 0)

    packed_out = lax.fori_loop(
        0, needed, attend_group, jnp.zeros((total_slots, block_width, half_width), jnp.bfloat16)
    )
    inverse = jnp.argsort(packing)
    attended_slots = jnp.take(packed_out, inverse, axis=0)
    returned = lax.all_to_all(
        attended_slots.reshape(sources, per_source, block_width, half_width),
        "users",
        split_axis=0,
        concat_axis=0,
        tiled=True,
    )
    prefix_part = jnp.take(returned.reshape(slot_count, block_width * half_width), position, axis=0)
    prefix_part = prefix_part.reshape(row_count, heads_here, HEAD_DIM).astype(jnp.float32)
    query_heads = queries.astype(jnp.float32).reshape(row_count, heads_here, HEAD_DIM)
    self_keys = activated[1].reshape(row_count, heads_here, HEAD_DIM)
    self_values = activated[2].reshape(row_count, heads_here, HEAD_DIM)
    own_term = (
        jax.nn.silu(jnp.sum(query_heads * self_keys, axis=-1) * score_scale)[..., None]
        * self_values
    )
    attended = (prefix_part + own_term).reshape(row_count, half_width)
    totals = lax.psum((jnp.sum(attended, axis=1), jnp.sum(attended * attended, axis=1)), "heads")
    row_mean = totals[0] / HD
    row_var = totals[1] / HD - row_mean * row_mean
    gated = (
        (attended - row_mean[:, None])
        * lax.rsqrt(row_var + EPSILON)[:, None]
        * attn_gain.astype(jnp.float32)
        * activated[3]
    ).astype(jnp.bfloat16)
    partial_out = jnp.dot(
        gated,
        lax.all_gather(w_o, "routers", axis=1, tiled=True),
        preferred_element_type=jnp.float32,
    )
    mixed = lax.psum(partial_out, "heads")
    residual = flat_items.astype(jnp.float32) + mixed
    row_scale = lax.rsqrt(jnp.sum(residual * residual, axis=1) / D + EPSILON)
    normed = (residual * row_scale[:, None] * mlp_gain.astype(jnp.float32)).astype(jnp.bfloat16)
    hidden = jax.nn.silu(jnp.dot(normed, w_one, preferred_element_type=jnp.float32)).astype(
        jnp.bfloat16
    )
    block_scores = jnp.dot(hidden, w_two, preferred_element_type=jnp.float32).reshape(
        blocks, block_width
    )
    is_valid = lax.broadcasted_iota(jnp.int32, (blocks, block_width), 1) < block_fill[:, None]
    return jnp.where(is_valid, block_scores, jnp.zeros_like(block_scores))


def solution(mesh):
    placed = (
        P(("groups", "users", "routers"), None, None),
        P(("groups", "users", "routers"), None),
        P(("groups", "users", "routers")),
        P(("groups", "users", "routers")),
        P(("groups", "users"), None, "heads"),
        P(("groups", "users"), None, "heads"),
        P(None, "routers", "heads"),
        P("heads"),
        P("heads", "routers"),
        P(),
        P(),
        P(),
    )
    return jax.shard_map(
        local,
        mesh=mesh,
        in_specs=placed,
        out_specs=P(("groups", "users", "routers"), None),
        check_vma=False,
    )
```

profile of v0, /device:TPU:0, one launch (start us, length us, event | category | flops | bytes accessed | tf_op | source)
XLA Modules:
  0.0 166.5 jit_solution(10524344665358077682)
XLA Ops:
  6.5 4.2 %copy.36 = bf16[4,512,512]{1,2,0:T(8,128)(2,1)} copy(bf16[4,512,512]{2,1,0:T(8,128)(2,1)} %param.24) | data formatting | bytes 4194304 | tf_op args[6]
  10.8 0.0 all-gather.3.cloned.1.call-update
  10.8 0.6 copy-done.10
  11.4 0.2 convert_reduce_fusion
  11.6 0.0 copy-done.12
  11.6 0.1 select_reduce_fusion
  11.7 0.7 sub.21
  12.4 6.3 %all-to-all-start = ((s32[4,1,2]{2,1,0:T(1,128)}), s32[4,1,2]{2,1,0:T(1,128)S(1)}, u32[]{:S(2)}, u32[]{:S(2)}) async-start(s32[4,1,2]{2,1,0:T(1,128)} %bitcast.5), calls=%async_computation | async-start | bytes 4096 | tf_op jit(solution)/shard_map/all_to_all | solution.py:76
  18.7 0.7 all-gather.5.cloned.1.call-update
  19.4 4.8 %all-to-all-done = s32[4,1,2]{2,1,0:T(1,128)S(1)} async-done(((s32[4,1,2]{2,1,0:T(1,128)}), s32[4,1,2]{2,1,0:T(1,128)S(1)}, u32[]{:S(2)}, u32[]{:S(2)}) %all-to-all-start) | async-done | bytes 64 | tf_op jit(solution)/shard_map/all_to_all | solution.py:76
  24.2 0.5 broadcast.235
  24.7 1.3 fusion.40
  26.0 0.1 reshape.118
  26.1 1.0 sort.34
  27.1 43.4 %all-gather.3.cloned.1.call-done = bf16[4,1024,512]{1,2,0:T(8,128)(2,1)} async-done(((bf16[4,512,512]{1,2,0:T(8,128)(2,1)}), bf16[4,1024,512]{1,2,0:T(8,128)(2,1)}) %all-gather.3.cloned.1.call-update) | async-done | bytes 4194320 | tf_op jit(solution)/shard_map/all_gather | solution.py:55
  70.4 0.0 copy-done.7
  70.4 3.6 %bitcast_multiply_fusion = f32[4,256,512]{1,2,0:T(8,128)S(1)} fusion(bf16[4,1024,512]{1,2,0:T(8,128)(2,1)} %all-gather.3.cloned.1.call-done, bf16[256,1024,1]{1,0,2:T(8,128)(2,1)S(1)} %bitcast.106), kind=kOutput, calls=%fused_computation.28 | convolution fusion | flops 1075838976 | bytes 6815744 | tf_op jit(solution)/shard_map/rk,pkc->prc/dot_general | solution.py:52
  74.0 0.0 copy-start.5
  74.0 1.3 copy-done.5
  75.4 0.9 slice_multiply_fusion
  76.3 0.1 copy.37
  76.4 0.2 convert_element_type.76
  76.6 0.4 convolution_convert_fusion.1
  77.0 1.0 copy.43
  78.0 4.7 %all-to-all-start.1 = ((bf16[4,2,64,512]{3,2,1,0:T(8,128)(2,1)}), bf16[4,2,64,512]{3,2,1,0:T(8,128)(2,1)S(1)}, u32[]{:S(2)}, u32[]{:S(2)}) async-start(bf16[4,2,64,512]{3,2,1,0:T(8,128)(2,1)} %bitcast.27), calls=%async_computation.1 | async-start | bytes 1048576 | tf_op jit(solution)/shard_map/all_to_all | solution.py:75
  83.4 0.6 gather_fusion.2
  84.0 1.0 sort.35
  85.0 12.0 %all-to-all-done.1 = bf16[4,2,64,512]{3,2,1,0:T(8,128)(2,1)S(1)} async-done(((bf16[4,2,64,512]{3,2,1,0:T(8,128)(2,1)}), bf16[4,2,64,512]{3,2,1,0:T(8,128)(2,1)S(1)}, u32[]{:S(2)}, u32[]{:S(2)}) %all-to-all-start.1) | async-done | bytes 524320 | tf_op jit(solution)/shard_map/all_to_all | solution.py:75
  97.0 0.6 gather_fusion.4
  97.6 0.9 broadcast_select_fusion.1
  98.6 0.9 broadcast_in_dim.66
  99.4 6.1 %while.10 = (s32[]{:T(128)}, bf16[8,64,512]{2,1,0:T(8,128)(2,1)}, s32[]{:T(128)}, s32[8]{0:T(128)S(1)}, bf16[2,256,512]{2,1,0:T(8,128)(2,1)S(1)}, /*index=5*/bf1...) while((s32[]{:T(128)}, bf16[8,64,512]{2,1,0:T(8,128)(2,1)}, ...), condition=%wide.region_5.8_spmd, body=%wide.region_4.7_spmd.sunk | while | flops 136971280 | bytes 13635875 | solution.py:94
  99.4 0.1 broadcast_compare_fusion.2
  99.5 0.6 gather_fusion
  100.1 0.6 gather_fusion.1
  100.7 1.5 select_bitcast_fusion.3
  102.3 2.5 %fusion.55 = bf16[4,4,8,8,128]{4,3,2,1,0:T(8,128)(2,1)S(1)} fusion(bf16[4,32,4,8,128]{4,3,2,1,0:T(8,128)(2,1)} %get-tuple-element.135, bf16[4,32,4,8,128]{4,3,2,1,0:T(8,128)(2,1)} %get-tuple-element.136, bf16[8,64,512]{2,1,0:T(8,128)(2,1)} %get-tuple-element.164, s32[]{:T(128)S(6)} %select_n.93), kind=kOutput, calls=%fused_computation.8.clone.1 | convolution fusion | flops 135921664 | bytes 2621444 | tf_op jit(solution)/shard_map/while/body/ghqk,gkhd->gqhd/dot_general | solution.py:26
  104.8 0.7 bitcast_dynamic-update-slice_fusion.2
  105.5 1.7 %gather_fusion.5 = bf16[8,64,512]{2,1,0:T(8,128)(2,1)S(1)} fusion(bf16[8,64,512]{2,1,0:T(8,128)(2,1)} %get-tuple-element.174, s32[1024]{0:T(1024)S(1)} %pad_clamp_fusion.2), kind=kCustom, calls=%fused_computation.2.clone | custom fusion | bytes 1048608 | tf_op jit(solution)/shard_map/jit(_take)/gather | solution.py:98
  107.2 0.9 broadcast_select_fusion
  108.1 3.5 %all-to-all-start.2 = ((bf16[4,2,64,512]{3,2,1,0:T(8,128)(2,1)}), bf16[4,2,64,512]{3,2,1,0:T(8,128)(2,1)S(1)}, u32[]{:S(2)}, u32[]{:S(2)}) async-start(bf16[4,2,64,512]{3,2,1,0:T(8,128)(2,1)} %bitcast.9), calls=%async_computation.2 | async-start | bytes 1048576 | tf_op jit(solution)/shard_map/all_to_all | solution.py:99
  111.6 0.0 all-reduce.3.cloned.1.call-start
  111.7 0.1 broadcast_in_dim.63
  111.8 0.1 broadcast_in_dim.64
  111.9 13.7 %all-to-all-done.2 = bf16[4,2,64,512]{3,2,1,0:T(8,128)(2,1)S(1)} async-done(((bf16[4,2,64,512]{3,2,1,0:T(8,128)(2,1)}), bf16[4,2,64,512]{3,2,1,0:T(8,128)(2,1)S(1)}, u32[]{:S(2)}, u32[]{:S(2)}) %all-to-all-start.2) | async-done | bytes 524320 | tf_op jit(solution)/shard_map/all_to_all | solution.py:99
  125.6 0.3 copy.44
  125.9 0.0 copy-start.6
  125.9 0.8 gather_fusion.3
  126.7 0.2 gather.18
  126.9 0.1 copy.38
  127.1 0.5 copy-done.6
  127.5 0.1 fusion.39
  127.7 2.5 %all-reduce = (f32[256]{0:T(256)S(1)}, f32[256]{0:T(256)S(1)}) all-reduce(f32[256]{0:T(256)S(1)} %get-tuple-element.51, f32[256]{0:T(256)S(1)} %get-tuple-element.50), channel_id=1, replica_groups=mesh['groups'=2,'users'=4,'routers'=2,'heads'=2] {'heads'}, use_global_device_ids=true, to_apply=%region_11.14 | all-reduce | flops 512 | bytes 4096 | tf_op jit(solution)/shard_map/psum | solution.py:116
  130.1 0.0 all-gather.5.cloned.1.call-done
  130.2 0.0 copy-start.9
  130.2 0.0 copy-start.14
  130.2 2.8 %fusion.27 = f32[256,1024]{1,0:T(8,128)} fusion(bf16[512,1024]{1,0:T(8,128)(2,1)} %all-gather.5.cloned.1.call-done, f32[4,256,512]{1,2,0:T(8,128)S(1)} %copy-done.6, f32[256,512]{0,1:T(8,128)S(1)} %get-tuple-element.72, f32[512]{0:T(512)S(1)} %convert_element_type.80, f32[256]{0:T(256)S(1)} %get-tuple-element.82, f32[256]{0:T(256)S(1)} %get-tuple-element.81), kind=kOutput, calls=%fused_computation.50 | convolution fusion | flops 269090816 | bytes 3149824 | tf_op jit(solution)/shard_map/dot_general | solution.py:125
  133.0 0.0 all-reduce.3.cloned.1.call-update
  133.0 0.0 copy-start.13
  133.1 22.9 %all-reduce.3.cloned.1.call-done = f32[256,1024]{1,0:T(8,128)} async-done(((f32[256,1024]{1,0:T(8,128)}), f32[256,1024]{1,0:T(8,128)}) %all-reduce.3.cloned.1.call-update) | async-done | bytes 1048592 | tf_op jit(solution)/shard_map/psum | solution.py:130
  155.9 1.6 multiply_reduce_fusion
  157.5 1.7 %fusion.29 = f32[1,256]{1,0:T(1,128)S(1)} fusion(bf16[256,1]{0,1:T(2,128)(2,1)S(1)} %reshape.186, bf16[1024,256]{1,0:T(8,128)(2,1)S(1)} %copy-done, f32[256,1024]{1,0:T(8,128)} %all-reduce.3.cloned.1.call-done, bf16[256,1024]{1,0:T(8,128)(2,1)S(1)} %bitcast.107, f32[1024]{0:T(1024)S(1)} %convert_element_type.82, f32[256]{0:T(256)S(1)} %add_rsqrt_fusion), kind=kOutput, calls=%fused_computation.52 | convolution fusion | flops 135987200 | bytes 2103808 | tf_op jit(solution)/shard_map/dot_general | solution.py:137
  159.2 0.1 reshape.123
  159.3 0.7 fusion.35
  (43 shorter events, 0.2 us)
Async XLA Ops:
  6.5 151.0 %copy-start = (bf16[1024,256]{1,0:T(8,128)(2,1)S(1)}, bf16[1024,256]{1,0:T(8,128)(2,1)}, u32[]{:S(2)}) copy-start(bf16[1024,256]{1,0:T(8,128)(2,1)} %param.28) | copy-start | bytes 1572868
  6.5 63.9 %all-gather.3.cloned.1.call-start = ((), (), s32[]{:S(2)}) async-start(), calls=%async_computation.3 | async-start | bytes 6291456 | tf_op jit(solution)/shard_map/all_gather | solution.py:55
  10.7 0.7 copy-start.10
  10.7 0.8 copy-start.12
  10.8 59.7 %copy-start.7 = (bf16[4,64,1024]{2,1,0:T(8,128)(2,1)S(1)}, bf16[4,64,1024]{2,1,0:T(8,128)(2,1)}, u32[]{:S(2)}) copy-start(bf16[4,64,1024]{2,1,0:T(8,128)(2,1)} %param.18) | copy-start | bytes 1572868
  12.4 11.8 %all-to-all-start = ((s32[4,1,2]{2,1,0:T(1,128)}), s32[4,1,2]{2,1,0:T(1,128)S(1)}, u32[]{:S(2)}, u32[]{:S(2)}) async-start(s32[4,1,2]{2,1,0:T(1,128)} %bitcast.5), calls=%async_computation | async-start | bytes 4096 | tf_op jit(solution)/shard_map/all_to_all | solution.py:76
  18.7 111.4 %all-gather.5.cloned.1.call-start = ((), (), s32[]{:S(2)}) async-start(), calls=%async_computation.4 | async-start | bytes 1572864 | tf_op jit(solution)/shard_map/all_gather | solution.py:127
  74.0 1.4 copy-start.5
  78.0 21.4 %copy-start.1 = (bf16[2,256,512]{2,1,0:T(8,128)(2,1)S(1)}, bf16[2,256,512]{2,1,0:T(8,128)(2,1)}, u32[]{:S(2)}) copy-start(bf16[2,256,512]{2,1,0:T(8,128)(2,1)} %param.23) | copy-start | bytes 1572868
  78.0 21.4 %copy-start.2 = (bf16[2,256,512]{2,1,0:T(8,128)(2,1)S(1)}, bf16[2,256,512]{2,1,0:T(8,128)(2,1)}, u32[]{:S(2)}) copy-start(bf16[2,256,512]{2,1,0:T(8,128)(2,1)} %param.22) | copy-start | bytes 1572868
  78.0 19.1 %all-to-all-start.1 = ((bf16[4,2,64,512]{3,2,1,0:T(8,128)(2,1)}), bf16[4,2,64,512]{3,2,1,0:T(8,128)(2,1)S(1)}, u32[]{:S(2)}, u32[]{:S(2)}) async-start(bf16[4,2,64,512]{3,2,1,0:T(8,128)(2,1)} %bitcast.27), calls=%async_computation.1 | async-start | bytes 1048576 | tf_op jit(solution)/shard_map/all_to_all | solution.py:75
  102.3 3.2 %copy-start.3 = (bf16[2,256,512]{2,1,0:T(8,128)(2,1)S(1)}, bf16[2,256,512]{2,1,0:T(8,128)(2,1)}, u32[]{:S(2)}) copy-start(bf16[2,256,512]{2,1,0:T(8,128)(2,1)} %get-tuple-element.184) | copy-start | bytes 1572868 | tf_op jit(solution)/shard_map/while
  105.5 6.3 %copy-start.11 = (bf16[512]{0:T(512)(128)(2,1)S(1)}, bf16[512]{0:T(512)(128)(2,1)}, u32[]{:S(2)}) copy-start(bf16[512]{0:T(512)(128)(2,1)} %param.25) | copy-start | bytes 3076
  105.5 6.3 %copy-start.4 = (f32[1,256,512]{1,2,0:T(8,128)S(1)}, f32[1,256,512]{1,2,0:T(8,128)}, u32[]{:S(2)}) copy-start(f32[1,256,512]{1,2,0:T(8,128)} %get-tuple-element.77) | copy-start | bytes 1572868
  108.1 17.5 %all-to-all-start.2 = ((bf16[4,2,64,512]{3,2,1,0:T(8,128)(2,1)}), bf16[4,2,64,512]{3,2,1,0:T(8,128)(2,1)S(1)}, u32[]{:S(2)}, u32[]{:S(2)}) async-start(bf16[4,2,64,512]{3,2,1,0:T(8,128)(2,1)} %bitcast.9), calls=%async_computation.2 | async-start | bytes 1048576 | tf_op jit(solution)/shard_map/all_to_all | solution.py:99
  111.6 44.3 %all-reduce.3.cloned.1.call-start = ((), (), s32[]{:S(2)}) async-start(), calls=%async_computation.5 | async-start | bytes 2097152 | tf_op jit(solution)/shard_map/psum | solution.py:130
  125.9 1.6 copy-start.6
  130.2 2.8 %copy-start.9 = (bf16[1024]{0:T(1024)(128)(2,1)S(1)}, bf16[1024]{0:T(1024)(128)(2,1)}, u32[]{:S(2)}) copy-start(bf16[1024]{0:T(1024)(128)(2,1)} %param.27) | copy-start | bytes 6148
  130.2 2.9 %copy-start.14 = (bf16[256]{0:T(256)(128)(2,1)S(1)}, bf16[256]{0:T(256)(128)(2,1)}, u32[]{:S(2)}) copy-start(bf16[256]{0:T(256)(128)(2,1)} %param.29) | copy-start | bytes 1540
  133.0 24.5 %copy-start.8 = (bf16[4,64,1024]{2,1,0:T(8,128)(2,1)S(1)}, bf16[4,64,1024]{2,1,0:T(8,128)(2,1)}, u32[]{:S(2)}) copy-start(bf16[4,64,1024]{2,1,0:T(8,128)(2,1)} %param.18) | copy-start | bytes 1572868
  133.0 26.3 %copy-start.13 = (s32[4]{0:T(128)S(1)}, s32[4]{0:T(128)}, u32[]{:S(2)}) copy-start(s32[4]{0:T(128)} %param.21) | copy-start | bytes 52
Sparse Core Ops, SparseCore 0:
  10.9 59.4 all-gather.2
  72.0 21.2 all-gather.4
  133.1 22.7 all-reduce.2
where the time goes:
time: 167 us; the launch traced here: 166 us
  waiting for transfers between devices  97.4 us (58%)
  local copies, waits for them, and re-layouts  16.6 us (10%)
  starting transfers between devices  14.6 us (9%)
  between operations  14 us (8%)
  matrix products  11 us (7%)
  other arithmetic  10.4 us (6%)
  blocking collectives  2.46 us (1%)
    all_gather x1, waiting for transfers between devices, local(): lax.all_gather(w_in, 'routers', axis=1, tiled=True)  43.4 us
    psum x1, waiting for transfers between devices, local(): mixed = lax.psum(partial_out, 'heads')  22.9 us
    all_to_all x1, waiting for transfers between devices, local(): lax.all_to_all(attended_slots.reshape(sources, per_source, block_width, h...  13.7 us
    all_to_all x1, waiting for transfers between devices, local(): lax.all_to_all(outgoing, 'users', split_axis=0, concat_axis=0, tiled=True)  12 us
    unnamed x32, local copies, waits for them, and re-layouts  7.95 us
    all_to_all x1, starting transfers between devices, local(): lax.all_to_all(slot_user, 'users', split_axis=0, concat_axis=0, tiled=True)  6.35 us
    all_to_all x1, waiting for transfers between devices, local(): lax.all_to_all(slot_user, 'users', split_axis=0, concat_axis=0, tiled=True)  4.76 us
    all_to_all x1, starting transfers between devices, local(): lax.all_to_all(outgoing, 'users', split_axis=0, concat_axis=0, tiled=True)  4.73 us
  transfers between devices with their start and end apart: 6, of which 5 were waited for; matrix products, arithmetic and copies ran while one was open for 15% of the time, Pallas kernels for 0%

commit v1 on v0

--- a/solution.py
+++ b/solution.py
@@ -2,6 +2,7 @@
 import jax.numpy as jnp
 from jax import lax
 from jax.sharding import PartitionSpec as P
+from jax.lax import axis_index, axis_size, ppermute
 
 D = 1024
 HEAD_DIM = 128
@@ -49,12 +50,28 @@
     slot_count = peer_count * CAP
     score_scale = HEAD_DIM ** (-0.5)
     flat_items = items.reshape(row_count, model_width)
+    later, field_out = (axis_size("routers"), axis_index("routers"))
+    panels = tuple(((to_i, (to_i - 1) % later) for to_i in range(later)))
+    built = w_in.shape[1]
+    local_part = w_in
     projected = jnp.einsum(
         "rk,pkc->prc",
-        flat_items,
-        lax.all_gather(w_in, "routers", axis=1, tiled=True),
+        lax.dynamic_slice_in_dim(flat_items, field_out * built, local_part.shape[1], axis=1),
+        local_part,
         preferred_element_type=jnp.float32,
     )
+    q = 1
+    while q < later:
+        local_part = ppermute(local_part, axis_name="routers", perm=panels)
+        projected = projected + jnp.einsum(
+            "rk,pkc->prc",
+            lax.dynamic_slice_in_dim(
+                flat_items, (field_out + q) % later * built, local_part.shape[1], axis=1
+            ),
+            local_part,
+            preferred_element_type=jnp.float32,
+        )
+        q = q + 1
     activated = jax.nn.silu(projected)
     queries = activated[0].astype(jnp.bfloat16)
     target = block_owner[:, 0]

time: 167 us -> 159 us (0.952)
  waiting for transfers between devices: 97.4 us -> 87.3 us
  local copies, waits for them, and re-layouts: 16.6 us -> 13.4 us
  starting transfers between devices: 14.6 us -> 16.6 us
  other arithmetic: 10.4 us -> 12.3 us
    all_gather x1 -> x0, waiting for transfers between devices: 43.4 us -> none  [local(): lax.all_gather(w_in, 'routers', axis=1, tiled=True)]
    ppermute x0 -> x1, waiting for transfers between devices: none -> 30.4 us  [local(): local_part = ppermute(local_part, axis_name='routers', perm=panels)]
    all_gather x1, waiting for transfers between devices: 0.01 us -> 10.1 us  [local(): lax.all_gather(w_o, 'routers', axis=1, tiled=True)]
    unnamed x32 -> x29, local copies, waits for them, and re-layouts: 7.95 us -> 2.64 us
    psum x1, waiting for transfers between devices: 22.9 us -> 19.5 us  [local(): mixed = lax.psum(partial_out, 'heads')]
    ppermute x0 -> x1, starting transfers between devices: none -> 2.97 us  [local(): local_part = ppermute(local_part, axis_name='routers', perm=panels)]
    all_to_all x1, waiting for transfers between devices: 4.76 us -> 3.05 us  [local(): lax.all_to_all(slot_user, 'users', split_axis=0, concat_axis=0, tiled=True)]
    dot_general x1 -> x2, matrix products: 3.6 us -> 4.87 us  [the longest x1 2.44 us: local(): jnp.einsum('rk,pkc->prc', lax.dynamic_slice_in_dim(flat_items, (field_out...]
  transfers between devices with their start and end apart: 6 -> 6, of which waited for: 5 -> 6; matrix products, arithmetic and copies ran while one was open for 15% -> 9% of each run, Pallas kernels for 0% -> 0%
where the time goes in v1:
time: 159 us
  waiting for transfers between devices  87.3 us (55%)
  starting transfers between devices  16.6 us (10%)
  between operations  14.3 us (9%)
  local copies, waits for them, and re-layouts  13.4 us (8%)
  other arithmetic  12.3 us (8%)
  matrix products  12.2 us (8%)
  blocking collectives  2.47 us (2%)
    ppermute x1, waiting for transfers between devices, local(): local_part = ppermute(local_part, axis_name='routers', perm=panels)  30.4 us
    psum x1, waiting for transfers between devices, local(): mixed = lax.psum(partial_out, 'heads')  19.5 us
    all_to_all x1, waiting for transfers between devices, local(): lax.all_to_all(attended_slots.reshape(sources, per_source, block_width, h...  12.2 us
    all_to_all x1, waiting for transfers between devices, local(): lax.all_to_all(outgoing, 'users', split_axis=0, concat_axis=0, tiled=True)  11.3 us
    all_gather x1, waiting for transfers between devices, local(): lax.all_gather(w_o, 'routers', axis=1, tiled=True)  10.1 us
    all_to_all x1, starting transfers between devices, local(): lax.all_to_all(outgoing, 'users', split_axis=0, concat_axis=0, tiled=True)  5.25 us
    all_to_all x1, starting transfers between devices, local(): lax.all_to_all(slot_user, 'users', split_axis=0, concat_axis=0, tiled=True)  4.87 us
    all_to_all x1, starting transfers between devices, local(): lax.all_to_all(attended_slots.reshape(sources, per_source, block_width, h...  3.47 us
  transfers between devices with their start and end apart: 6, of which 6 were waited for; matrix products, arithmetic and copies ran while one was open for 9% of the time, Pallas kernels for 0%

profile of v1, /device:TPU:0, one launch (start us, length us, event | category | flops | bytes accessed | tf_op | source)
XLA Modules:
  0.0 158.7 jit_solution(14207532608884626713)
XLA Ops:
  6.5 3.0 %collective-permute-start = (bf16[4,512,512]{2,1,0:T(8,128)(2,1)}, bf16[4,512,512]{2,1,0:T(8,128)(2,1)}, u32[]{:S(2)}, u32[]{:S(2)}) collective-permute-start(bf16[4,512,512]{2,1,0:T(8,128)(2,1)} %param.24), channel_id=1, source_target_pairs={{0,2},{2,0},{1,3},{3,1},{4,6},{6,4},{5,7},{7,5},{8,10},{10,8},{9,1... | collective-permute-start | bytes 6291464 | tf_op jit(solution)/shard_map/ppermute | solution.py:65
  9.5 0.9 convert_reduce_fusion
  10.4 0.7 multiply_add_fusion
  11.1 0.1 select_reduce_fusion
  11.2 0.7 sub.21
  11.9 4.9 %all-to-all-start = ((s32[4,1,2]{2,1,0:T(1,128)}), s32[4,1,2]{2,1,0:T(1,128)S(1)}, u32[]{:S(2)}, u32[]{:S(2)}) async-start(s32[4,1,2]{2,1,0:T(1,128)} %bitcast.5), calls=%async_computation | async-start | bytes 4096 | tf_op jit(solution)/shard_map/all_to_all | solution.py:93
  16.7 2.4 %fusion.29 = f32[256,4,512]{2,0,1:T(8,128)S(1)} fusion(bf16[4,512,512]{2,1,0:T(8,128)(2,1)} %param.24, bf16[256,1024]{1,0:T(8,128)(2,1)} %bitcast.110, s32[]{:T(128)S(6)} %select_n.70), kind=kOutput, calls=%fused_computation.52 | convolution fusion | flops 536870912 | bytes 4456452 | tf_op jit(solution)/shard_map/rk,pkc->prc/dot_general | solution.py:57
  19.2 3.1 %all-to-all-done = s32[4,1,2]{2,1,0:T(1,128)S(1)} async-done(((s32[4,1,2]{2,1,0:T(1,128)}), s32[4,1,2]{2,1,0:T(1,128)S(1)}, u32[]{:S(2)}, u32[]{:S(2)}) %all-to-all-start) | async-done | bytes 64 | tf_op jit(solution)/shard_map/all_to_all | solution.py:93
  22.2 0.5 broadcast.236
  22.7 1.3 fusion.46
  24.0 0.1 reshape.118
  24.1 1.0 sort.34
  25.1 30.4 %collective-permute-done = bf16[4,512,512]{2,1,0:T(8,128)(2,1)} collective-permute-done((bf16[4,512,512]{2,1,0:T(8,128)(2,1)}, bf16[4,512,512]{2,1,0:T(8,128)(2,1)}, u32[]{:S(2)}, u32[]{:S(2)}) %collective-permute-start) | collective-permute-done | bytes 2097184 | tf_op jit(solution)/shard_map/ppermute | solution.py:65
  55.4 0.0 copy-done.7
  55.4 2.4 %bitcast_multiply_fusion = f32[4,256,512]{2,1,0:T(8,128)S(1)} fusion(f32[256,4,512]{2,0,1:T(8,128)S(1)} %fusion.29, bf16[4,512,512]{2,1,0:T(8,128)(2,1)} %collective-permute-done, bf16[256,1024]{1,0:T(8,128)(2,1)S(1)} %bitcast.111, s32[]{:T(128)S(6)} %select_n.72), kind=kOutput, calls=%fused_computation.28 | convolution fusion | flops 539492352 | bytes 6553604 | tf_op jit(solution)/shard_map/rk,pkc->prc/dot_general | solution.py:66
  57.9 0.0 copy-start.5
  57.9 1.3 copy-done.5
  59.2 0.9 slice_multiply_fusion
  60.1 0.2 convert_element_type.76
  60.3 0.4 convolution_convert_fusion.1
  60.7 1.0 copy.46
  61.7 5.3 %all-to-all-start.1 = ((bf16[4,2,64,512]{3,2,1,0:T(8,128)(2,1)}), bf16[4,2,64,512]{3,2,1,0:T(8,128)(2,1)S(1)}, u32[]{:S(2)}, u32[]{:S(2)}) async-start(bf16[4,2,64,512]{3,2,1,0:T(8,128)(2,1)} %bitcast.25), calls=%async_computation.1 | async-start | bytes 1048576 | tf_op jit(solution)/shard_map/all_to_all | solution.py:92
  67.6 0.6 gather_fusion.2
  68.3 1.0 sort.35
  69.3 11.3 %all-to-all-done.1 = bf16[4,2,64,512]{3,2,1,0:T(8,128)(2,1)S(1)} async-done(((bf16[4,2,64,512]{3,2,1,0:T(8,128)(2,1)}), bf16[4,2,64,512]{3,2,1,0:T(8,128)(2,1)S(1)}, u32[]{:S(2)}, u32[]{:S(2)}) %all-to-all-start.1) | async-done | bytes 524320 | tf_op jit(solution)/shard_map/all_to_all | solution.py:92
  80.6 0.6 gather_fusion.4
  81.2 0.9 broadcast_select_fusion.1
  82.1 0.9 broadcast_in_dim.66
  83.0 6.1 %while.10 = (s32[]{:T(128)}, bf16[8,64,512]{2,1,0:T(8,128)(2,1)}, s32[]{:T(128)}, s32[8]{0:T(128)S(1)}, bf16[2,256,512]{2,1,0:T(8,128)(2,1)S(1)}, /*index=5*/bf1...) while((s32[]{:T(128)}, bf16[8,64,512]{2,1,0:T(8,128)(2,1)}, ...), condition=%wide.region_5.8_spmd, body=%wide.region_4.7_spmd.sunk | while | flops 136971280 | bytes 13635875 | solution.py:111
  83.0 0.1 broadcast_compare_fusion.2
  83.1 0.6 gather_fusion
  83.7 0.6 gather_fusion.1
  84.3 1.5 select_bitcast_fusion.3
  85.8 2.5 %fusion.61 = bf16[4,4,8,8,128]{4,3,2,1,0:T(8,128)(2,1)S(1)} fusion(bf16[4,32,4,8,128]{4,3,2,1,0:T(8,128)(2,1)} %get-tuple-element.135, bf16[4,32,4,8,128]{4,3,2,1,0:T(8,128)(2,1)} %get-tuple-element.136, bf16[8,64,512]{2,1,0:T(8,128)(2,1)} %get-tuple-element.164, s32[]{:T(128)S(6)} %select_n.108), kind=kOutput, calls=%fused_computation.8.clone.1 | convolution fusion | flops 135921664 | bytes 2621444 | tf_op jit(solution)/shard_map/while/body/ghqk,gkhd->gqhd/dot_general | solution.py:27
  88.3 0.7 bitcast_dynamic-update-slice_fusion.2
  89.1 1.7 %gather_fusion.5 = bf16[8,64,512]{2,1,0:T(8,128)(2,1)S(1)} fusion(bf16[8,64,512]{2,1,0:T(8,128)(2,1)} %get-tuple-element.173, s32[1024]{0:T(1024)S(1)} %pad_clamp_fusion.2), kind=kCustom, calls=%fused_computation.2.clone | custom fusion | bytes 1048608 | tf_op jit(solution)/shard_map/jit(_take)/gather | solution.py:115
  90.8 0.9 broadcast_select_fusion
  91.7 3.5 %all-to-all-start.2 = ((bf16[4,2,64,512]{3,2,1,0:T(8,128)(2,1)}), bf16[4,2,64,512]{3,2,1,0:T(8,128)(2,1)S(1)}, u32[]{:S(2)}, u32[]{:S(2)}) async-start(bf16[4,2,64,512]{3,2,1,0:T(8,128)(2,1)} %bitcast.10), calls=%async_computation.2 | async-start | bytes 1048576 | tf_op jit(solution)/shard_map/all_to_all | solution.py:116
  95.1 0.0 all-gather.2.cloned.1.call-start
  95.2 0.7 all-gather.2.cloned.1.call-update
  95.9 0.0 all-reduce.3.cloned.1.call-start
  95.9 0.0 copy-done.10
  95.9 0.1 broadcast_in_dim.63
  96.0 0.1 broadcast_in_dim.64
  96.1 0.2 mul.124
  96.3 0.3 reduce_sum.69
  96.7 0.1 copy.40
  96.8 0.1 copy.41
  96.9 12.2 %all-to-all-done.2 = bf16[4,2,64,512]{3,2,1,0:T(8,128)(2,1)S(1)} async-done(((bf16[4,2,64,512]{3,2,1,0:T(8,128)(2,1)}), bf16[4,2,64,512]{3,2,1,0:T(8,128)(2,1)S(1)}, u32[]{:S(2)}, u32[]{:S(2)}) %all-to-all-start.2) | async-done | bytes 524320 | tf_op jit(solution)/shard_map/all_to_all | solution.py:116
  109.2 0.3 copy.47
  109.5 1.5 gather_fusion.3
  111.0 1.1 gather.18
  112.1 0.3 mul.128
  112.5 0.3 fusion.45
  112.8 2.5 %all-reduce = (f32[256]{0:T(256)S(1)}, f32[256]{0:T(256)S(1)}) all-reduce(f32[256]{0:T(256)S(1)} %get-tuple-element.51, f32[256]{0:T(256)S(1)} %get-tuple-element.50), channel_id=1, replica_groups=mesh['groups'=2,'users'=4,'routers'=2,'heads'=2] {'heads'}, use_global_device_ids=true, to_apply=%region_11.14 | all-reduce | flops 512 | bytes 4096 | tf_op jit(solution)/shard_map/psum | solution.py:133
  115.3 10.1 %all-gather.2.cloned.1.call-done = bf16[512,1024]{1,0:T(8,128)(2,1)} async-done(((bf16[512,512]{1,0:T(8,128)(2,1)}), bf16[512,1024]{1,0:T(8,128)(2,1)}) %all-gather.2.cloned.1.call-update) | async-done | bytes 1048592 | tf_op jit(solution)/shard_map/all_gather | solution.py:144
  125.4 2.7 %fusion.26 = f32[256,1024]{1,0:T(8,128)} fusion(bf16[512,1024]{1,0:T(8,128)(2,1)} %all-gather.2.cloned.1.call-done, f32[4,256,512]{2,1,0:T(8,128)S(1)} %copy-done.6, f32[256,512]{1,0:T(8,128)S(1)} %get-tuple-element.72, f32[512]{0:T(512)S(1)} %convert_element_type.80, f32[256]{0:T(256)S(1)} %get-tuple-element.82, f32[256]{0:T(256)S(1)} %get-tuple-element.81), kind=kOutput, calls=%fused_computation.50 | convolution fusion | flops 269090816 | bytes 3149824 | tf_op jit(solution)/shard_map/dot_general | solution.py:142
  128.1 0.0 all-reduce.3.cloned.1.call-update
  128.2 0.0 copy-start.12
  128.2 19.5 %all-reduce.3.cloned.1.call-done = f32[256,1024]{1,0:T(8,128)} async-done(((f32[256,1024]{1,0:T(8,128)}), f32[256,1024]{1,0:T(8,128)}) %all-reduce.3.cloned.1.call-update) | async-done | bytes 1048592 | tf_op jit(solution)/shard_map/psum | solution.py:147
  147.7 1.6 multiply_reduce_fusion
  149.3 1.7 %fusion.31 = f32[1,256]{1,0:T(1,128)S(1)} fusion(bf16[256,1]{0,1:T(2,128)(2,1)S(1)} %reshape.187, bf16[1024,256]{1,0:T(8,128)(2,1)S(1)} %copy-done, f32[256,1024]{1,0:T(8,128)} %all-reduce.3.cloned.1.call-done, bf16[256,1024]{1,0:T(8,128)(2,1)S(1)} %bitcast.112, f32[1024]{0:T(1024)S(1)} %convert_element_type.82, f32[256]{0:T(256)S(1)} %add_rsqrt_fusion), kind=kOutput, calls=%fused_computation.55 | convolution fusion | flops 135987200 | bytes 2103808 | tf_op jit(solution)/shard_map/dot_general | solution.py:154
  151.1 0.1 reshape.123
  151.2 0.7 fusion.39
  (42 shorter events, 0.2 us)
Async XLA Ops:
  6.5 142.8 %copy-start = (bf16[1024,256]{1,0:T(8,128)(2,1)S(1)}, bf16[1024,256]{1,0:T(8,128)(2,1)}, u32[]{:S(2)}) copy-start(bf16[1024,256]{1,0:T(8,128)(2,1)} %param.28) | copy-start | bytes 1572868
  6.5 48.9 %collective-permute-start = (bf16[4,512,512]{2,1,0:T(8,128)(2,1)}, bf16[4,512,512]{2,1,0:T(8,128)(2,1)}, u32[]{:S(2)}, u32[]{:S(2)}) collective-permute-start(bf16[4,512,512]{2,1,0:T(8,128)(2,1)} %param.24), channel_id=1, source_target_pairs={{0,2},{2,0},{1,3},{3,1},{4,6},{6,4},{5,7},{7,5},{8,10},{10,8},{9,1... | collective-permute-start | bytes 6291464 | tf_op jit(solution)/shard_map/ppermute | solution.py:65
  11.9 10.4 %all-to-all-start = ((s32[4,1,2]{2,1,0:T(1,128)}), s32[4,1,2]{2,1,0:T(1,128)S(1)}, u32[]{:S(2)}, u32[]{:S(2)}) async-start(s32[4,1,2]{2,1,0:T(1,128)} %bitcast.5), calls=%async_computation | async-start | bytes 4096 | tf_op jit(solution)/shard_map/all_to_all | solution.py:93
  16.7 38.7 %copy-start.7 = (bf16[4,64,1024]{2,1,0:T(8,128)(2,1)S(1)}, bf16[4,64,1024]{2,1,0:T(8,128)(2,1)}, u32[]{:S(2)}) copy-start(bf16[4,64,1024]{2,1,0:T(8,128)(2,1)} %param.18) | copy-start | bytes 1572868
  57.9 1.4 copy-start.5
  61.7 21.3 %copy-start.1 = (bf16[2,256,512]{2,1,0:T(8,128)(2,1)S(1)}, bf16[2,256,512]{2,1,0:T(8,128)(2,1)}, u32[]{:S(2)}) copy-start(bf16[2,256,512]{2,1,0:T(8,128)(2,1)} %param.23) | copy-start | bytes 1572868
  61.7 21.3 %copy-start.2 = (bf16[2,256,512]{2,1,0:T(8,128)(2,1)S(1)}, bf16[2,256,512]{2,1,0:T(8,128)(2,1)}, u32[]{:S(2)}) copy-start(bf16[2,256,512]{2,1,0:T(8,128)(2,1)} %param.22) | copy-start | bytes 1572868
  61.7 18.9 %all-to-all-start.1 = ((bf16[4,2,64,512]{3,2,1,0:T(8,128)(2,1)}), bf16[4,2,64,512]{3,2,1,0:T(8,128)(2,1)S(1)}, u32[]{:S(2)}, u32[]{:S(2)}) async-start(bf16[4,2,64,512]{3,2,1,0:T(8,128)(2,1)} %bitcast.25), calls=%async_computation.1 | async-start | bytes 1048576 | tf_op jit(solution)/shard_map/all_to_all | solution.py:92
  85.8 3.2 %copy-start.3 = (bf16[2,256,512]{2,1,0:T(8,128)(2,1)S(1)}, bf16[2,256,512]{2,1,0:T(8,128)(2,1)}, u32[]{:S(2)}) copy-start(bf16[2,256,512]{2,1,0:T(8,128)(2,1)} %get-tuple-element.183) | copy-start | bytes 1572868 | tf_op jit(solution)/shard_map/while
  89.1 6.9 %copy-start.10 = (s32[4,1]{0,1:T(1,128)S(1)}, s32[4,1]{0,1:T(1,128)}, u32[]{:S(2)}) copy-start(s32[4,1]{0,1:T(1,128)} %param.19) | copy-start | bytes 52
  89.1 7.1 %copy-start.11 = (bf16[512]{0:T(512)(128)(2,1)S(1)}, bf16[512]{0:T(512)(128)(2,1)}, u32[]{:S(2)}) copy-start(bf16[512]{0:T(512)(128)(2,1)} %param.25) | copy-start | bytes 3076
  89.1 7.1 %copy-start.4 = (f32[1,256,512]{2,1,0:T(8,128)S(1)}, f32[1,256,512]{2,1,0:T(8,128)}, u32[]{:S(2)}) copy-start(f32[1,256,512]{2,1,0:T(8,128)} %get-tuple-element.77) | copy-start | bytes 1572868
  91.7 17.5 %all-to-all-start.2 = ((bf16[4,2,64,512]{3,2,1,0:T(8,128)(2,1)}), bf16[4,2,64,512]{3,2,1,0:T(8,128)(2,1)S(1)}, u32[]{:S(2)}, u32[]{:S(2)}) async-start(bf16[4,2,64,512]{3,2,1,0:T(8,128)(2,1)} %bitcast.10), calls=%async_computation.2 | async-start | bytes 1048576 | tf_op jit(solution)/shard_map/all_to_all | solution.py:116
  95.1 30.2 %all-gather.2.cloned.1.call-start = ((), (), s32[]{:S(2)}) async-start(), calls=%async_computation.3 | async-start | bytes 1572864 | tf_op jit(solution)/shard_map/all_gather | solution.py:144
  95.9 51.9 %all-reduce.3.cloned.1.call-start = ((), (), s32[]{:S(2)}) async-start(), calls=%async_computation.4 | async-start | bytes 2097152 | tf_op jit(solution)/shard_map/psum | solution.py:147
  109.5 3.0 %copy-start.6 = (f32[4,256,512]{2,1,0:T(8,128)S(1)}, f32[4,256,512]{2,1,0:T(8,128)}, u32[]{:S(2)}) copy-start(f32[4,256,512]{2,1,0:T(8,128)} %copy-done.5) | copy-start | bytes 6291460
  125.4 2.8 %copy-start.9 = (bf16[1024]{0:T(1024)(128)(2,1)S(1)}, bf16[1024]{0:T(1024)(128)(2,1)}, u32[]{:S(2)}) copy-start(bf16[1024]{0:T(1024)(128)(2,1)} %param.27) | copy-start | bytes 6148
  125.4 2.8 %copy-start.13 = (bf16[256]{0:T(256)(128)(2,1)S(1)}, bf16[256]{0:T(256)(128)(2,1)}, u32[]{:S(2)}) copy-start(bf16[256]{0:T(256)(128)(2,1)} %param.29) | copy-start | bytes 1540
  128.1 21.2 %copy-start.8 = (bf16[4,64,1024]{2,1,0:T(8,128)(2,1)S(1)}, bf16[4,64,1024]{2,1,0:T(8,128)(2,1)}, u32[]{:S(2)}) copy-start(bf16[4,64,1024]{2,1,0:T(8,128)(2,1)} %param.18) | copy-start | bytes 1572868
  128.2 23.0 %copy-start.12 = (s32[4]{0:T(128)S(1)}, s32[4]{0:T(128)}, u32[]{:S(2)}) copy-start(s32[4]{0:T(128)} %param.21) | copy-start | bytes 52
Sparse Core Ops, SparseCore 0:
  97.5 27.8 all-gather.1
  128.3 19.4 all-reduce.2
